TPU v7x, 32 devices: a whole 2x2x4 slice. The times are simulated.
32 devices in a mesh: seq: 8 (over z, y), head: 4 (over x, core).
Axes of the slice: x: 2, y: 2, z: 4, core: 2. Of those that a mesh axis runs over, the one named last changes fastest.
Arguments:
- query: bfloat16 [512, 2048], P('seq', 'head'), may hold values from -16 to 16
- key_states: bfloat16 [512, 2048], P('seq', 'head'), may hold values from -16 to 16
- value_states: bfloat16 [512, 2048], P('seq', 'head'), may hold values from -6 to 6
- doc_ids: int32 [512], P('seq'), may hold values from 0 to 3, never falling along the last dimension, each value on 1 to 256 neighbouring positions
- out_weight: bfloat16 [2048, 4096], P('head', 'seq'), may hold values from -0.1875 to 0.1875
- residual: bfloat16 [512, 4096], P('seq', 'head'), may hold values from -6 to 6
Outputs:
- mixed: bfloat16 [512, 4096], P('seq', 'head')
Inputs may be any that keep to these rules, and one draw needn't show every extreme that they name: doc_ids never fall along the sequence; every document has 1 to 256 positions, and one has exactly 256.
All inputs are finite; a program needn't handle non-finite values.
Results may differ from a plain program's by a relative error of at most 0.0055.
Values may be sent and summed in bfloat16 or wider, within the bound.
A program may use at most 64 MiB of HBM per device.

v0:
```python
import jax
import jax.numpy as jnp
from jax import lax
from jax.sharding import PartitionSpec as P

HEAD_DIM = 128
masked_score = -1e30


def to_heads(block):
    return block.reshape(block.shape[0], block.shape[1] // HEAD_DIM, HEAD_DIM)


def attend_block(state, queries, query_pos, query_docs, keys, values, key_pos, key_docs):
    run_max, run_sum, run_acc = state
    scores = jnp.einsum(
        "qhd,khd->hqk", queries, keys, preferred_element_type=jnp.float32
    ) * HEAD_DIM ** (-0.5)
    allowed = (key_pos[None, :] <= query_pos[:, None]) & (key_docs[None, :] == query_docs[:, None])
    scores = jnp.where(allowed[None], scores, masked_score)
    new_max = jnp.maximum(run_max, jnp.max(scores, axis=-1))
    weights = jnp.where(allowed[None], jnp.exp(scores - new_max[..., None]), 0.0)
    run_sum = jnp.sum(weights, axis=-1)
    run_acc = jnp.einsum(
        "hqk,khd->hqd", weights.astype(jnp.bfloat16), values, preferred_element_type=jnp.float32
    )
    return (new_max, run_sum, run_acc)


def shards(query, key_states, value_states, doc_ids, out_weight, residual):
    tok_rows = query.shape[0]
    heads = query.shape[1] // HEAD_DIM
    shard_index = lax.axis_index("seq")
    first_pos = shard_index * tok_rows
    groups = [(query, first_pos + jnp.arange(tok_rows, dtype=jnp.int32), doc_ids)]
    prepared = [(to_heads(block), block_pos, block_docs) for block, block_pos, block_docs in groups]
    initial = tuple(
        (
            (
                jnp.full((heads, block_pos.shape[0]), masked_score, jnp.float32),
                jnp.zeros((heads, block_pos.shape[0]), jnp.float32),
                jnp.zeros((heads, block_pos.shape[0], HEAD_DIM), jnp.float32),
            )
            for block, block_pos, block_docs in groups
        )
    )
    first_row = jnp.int32(0)
    keys = lax.all_gather(key_states, "seq", axis=0, tiled=True)
    values = lax.all_gather(value_states, "seq", axis=0, tiled=True)
    key_docs = lax.all_gather(doc_ids, "seq", axis=0, tiled=True)
    key_pos = jnp.arange(keys.shape[0], dtype=jnp.int32)
    key_heads = to_heads(keys)
    value_heads = to_heads(values)
    updated = []
    for member, state in zip(prepared, initial):
        queries, query_pos, query_docs = member

        def advance(inner, queries=queries, query_pos=query_pos, query_docs=query_docs):
            return attend_block(
                inner, queries, query_pos, query_docs, key_heads, value_heads, key_pos, key_docs
            )

        def unchanged(inner):
            return inner

        updated.append(lax.cond(first_row <= jnp.max(query_pos), advance, unchanged, state))
    finals = tuple(updated)
    outputs = []
    for run_max, run_sum, run_acc in finals:
        normed = run_acc / run_sum[..., None]
        outputs.append(
            jnp.transpose(normed, (1, 0, 2))
            .reshape(normed.shape[1], heads * HEAD_DIM)
            .astype(jnp.bfloat16)
        )
    attended = outputs[0]
    mapped = jnp.dot(
        attended,
        lax.all_gather(out_weight, "seq", axis=1, tiled=True),
        preferred_element_type=jnp.float32,
    )
    summed = lax.psum_scatter(mapped, "head", scatter_dimension=1, tiled=True)
    return (residual.astype(jnp.float32) + summed).astype(jnp.bfloat16)


def solution(mesh):
    placed = (
        P("seq", "head"),
        P("seq", "head"),
        P("seq", "head"),
        P("seq"),
        P("head", "seq"),
        P("seq", "head"),
    )
    return jax.shard_map(
        shards, mesh=mesh, in_specs=placed, out_specs=P("seq", "head"), check_vma=False
    )
```

profile of v0, /device:TPU:0, one launch (start us, length us, event | category | flops | bytes accessed | tf_op | source)
XLA Modules:
  0.0 137.0 jit_solution(2854361127337461728)
XLA Ops:
  6.5 0.0 all-gather.2.cloned.1.call-start
  6.5 0.7 all-gather.2.cloned.1.call-update
  7.3 0.0 reduce-scatter.2.cloned.1.call-start
  7.3 0.6 fusion.19
  8.6 1.3 dynamic-slice
  10.5 0.9 dynamic-update-slice
  11.3 13.2 %all-reduce = s32[512]{0:T(512)S(1)} all-reduce(s32[512]{0:T(512)S(1)} %dynamic-update-slice), channel_id=1, replica_groups=mesh['seq'=8,'head'=4] {'seq'}, use_global_device_ids=true, to_apply=%add | all-reduce | flops 512 | bytes 4096
  24.5 33.5 %all_gather.13 = bf16[512,512]{1,0:T(8,128)(2,1)S(1)} all-gather(bf16[64,512]{1,0:T(8,128)(2,1)} %param.9), channel_id=1, replica_groups=mesh['seq'=8,'head'=4] {'seq'}, dimensions={0}, use_global_device_ids=true | all-gather | bytes 589824 | tf_op jit(solution)/shard_map/all_gather | solution.py:48
  58.1 33.8 %all_gather.14 = bf16[512,512]{1,0:T(8,128)(2,1)S(1)} all-gather(bf16[64,512]{1,0:T(8,128)(2,1)} %param.10), channel_id=1, replica_groups=mesh['seq'=8,'head'=4] {'seq'}, dimensions={0}, use_global_device_ids=true | all-gather | bytes 589824 | tf_op jit(solution)/shard_map/all_gather | solution.py:49
  91.8 0.0 copy-start
  91.8 2.6 %conditional.1 = (f32[4,64]{1,0:T(4,128)S(1)}, f32[4,64,128]{2,1,0:T(8,128)S(1)}) conditional(s32[]{:T(128)} %convert_element_type.22, () %tuple.13, (s32[512]{0:T(512)S(1)}, s32[64]{0:T(128)S(1)}, s32[512]{0:T(512)S(1)}, s32[64]{0:T(128)}, bf16[64,512]{1,0:T(8,128)(2,1)}, /*index=5*/bf16[512,512]{1,0:T(8,128)(2,1)S(1)}, ...), branch_computations={%region_1.0_spmd, %region_2.5_spmd} | conditional | flops 68386560 | bytes 2959888 | solution.py:66
  91.8 0.8 compare_and_fusion
  92.6 1.2 fusion.20
  93.9 0.3 fusion.1
  94.2 0.2 fusion.7
  94.4 5.8 %all-gather.2.cloned.1.call-done = bf16[512,4096]{1,0:T(8,128)(2,1)} async-done(((bf16[512,512]{1,0:T(8,128)(2,1)}), bf16[512,4096]{1,0:T(8,128)(2,1)}) %all-gather.2.cloned.1.call-update) | async-done | bytes 4194320 | tf_op jit(solution)/shard_map/all_gather | solution.py:79
  100.2 4.1 %fusion.15 = f32[64,4096]{1,0:T(8,128)} fusion(bf16[512,4096]{1,0:T(8,128)(2,1)} %all-gather.2.cloned.1.call-done, f32[4,64,128]{2,1,0:T(8,128)S(1)} %get-tuple-element.31, f32[4,64]{1,0:T(4,128)S(1)} %get-tuple-element.32), kind=kOutput, calls=%fused_computation.20 | convolution fusion | flops 268500992 | bytes 5374976 | tf_op jit(solution)/shard_map/dot_general | solution.py:77
  104.2 0.0 reduce-scatter.2.cloned.1.call-update
  104.2 24.2 %reduce-scatter.2.cloned.1.call-done = f32[64,1024]{1,0:T(8,128)} async-done(((f32[64,4096]{1,0:T(8,128)}), f32[64,1024]{1,0:T(8,128)}) %reduce-scatter.2.cloned.1.call-update) | async-done | bytes 262160 | tf_op jit(solution)/shard_map/reduce_scatter | solution.py:82
  128.5 0.0 copy-done
  128.5 1.6 %add_convert_fusion = bf16[64,1024]{1,0:T(8,128)(2,1)} fusion(f32[64,1024]{1,0:T(8,128)} %reduce-scatter.2.cloned.1.call-done, bf16[64,1024]{1,0:T(8,128)(2,1)S(1)} %copy-done), kind=kLoop, calls=%fused_computation.18 | loop fusion | flops 196608 | bytes 524288 | tf_op jit(solution)/shard_map/convert_element_type | solution.py:83
  (4 shorter events, 0.0 us)
Async XLA Ops:
  6.5 93.6 %all-gather.2.cloned.1.call-start = ((), (), s32[]{:S(2)}) async-start(), calls=%async_computation.1 | async-start | bytes 4718592 | tf_op jit(solution)/shard_map/all_gather | solution.py:79
  7.3 121.2 %reduce-scatter.2.cloned.1.call-start = ((), (), s32[]{:S(2)}) async-start(), calls=%async_computation.2 | async-start | bytes 1310720 | tf_op jit(solution)/shard_map/reduce_scatter | solution.py:82
  91.8 36.7 %copy-start = (bf16[64,1024]{1,0:T(8,128)(2,1)S(1)}, bf16[64,1024]{1,0:T(8,128)(2,1)}, u32[]{:S(2)}) copy-start(bf16[64,1024]{1,0:T(8,128)(2,1)} %param.13) | copy-start | bytes 393220
Sparse Core Ops, SparseCore 0:
  9.4 90.7 all-gather.1
  104.4 24.0 reduce-scatter.1
where the time goes:
time: 137 us
  blocking collectives  80.5 us (59%)
  waiting for transfers between devices  30.7 us (22%)
  between operations  14.7 us (11%)
  matrix products  5.57 us (4%)
  other arithmetic  3.29 us (2%)
  local copies, waits for them, and re-layouts  2.12 us (2%)
    all_gather x1, blocking collectives, shards(): values = lax.all_gather(value_states, 'seq', axis=0, tiled=True)  33.8 us
    all_gather x1, blocking collectives, shards(): keys = lax.all_gather(key_states, 'seq', axis=0, tiled=True)  33.5 us
    reduce_scatter x1, waiting for transfers between devices, shards(): summed = lax.psum_scatter(mapped, 'head', scatter_dimension=1, tiled=True)  24.2 us
    unnamed x1, blocking collectives  13.2 us
    all_gather x1, waiting for transfers between devices, shards(): lax.all_gather(out_weight, 'seq', axis=1, tiled=True)  5.75 us
    dot_general x1, matrix products, shards(): jnp.dot(attended, lax.all_gather(out_weight, 'seq', axis=1, tiled=True),...  4.06 us
  transfers between devices with their start and end apart: 2, of which 2 were waited for; matrix products, arithmetic and copies ran while one was open for 4% of the time, Pallas kernels for 0%

commit v1 on v0

--- a/solution.py
+++ b/solution.py
@@ -5,6 +5,23 @@
 
 HEAD_DIM = 128
 masked_score = -1e30
+
+
+def joined_along(blocks, dim):
+    blocks = jnp.moveaxis(blocks, 0, dim)
+    lengths = blocks.shape
+    return blocks.reshape(*lengths[:dim], lengths[dim] * lengths[dim + 1], *lengths[dim + 2 :])
+
+
+def ring_gather(x, axis, dim):
+    size = lax.axis_size(axis)
+    ahead = [(i, (i + 1) % size) for i in range(size)]
+    blocks = [x]
+    while len(blocks) < size:
+        blocks.append(lax.ppermute(blocks[-1], axis, ahead))
+    here = lax.axis_index(axis)
+    blocks = jnp.stack(blocks)[(here - jnp.arange(size)) % size]
+    return joined_along(blocks, dim)
 
 
 def to_heads(block):
@@ -46,7 +63,7 @@
     )
     first_row = jnp.int32(0)
     keys = lax.all_gather(key_states, "seq", axis=0, tiled=True)
-    values = lax.all_gather(value_states, "seq", axis=0, tiled=True)
+    values = ring_gather(value_states, "seq", 0)
     key_docs = lax.all_gather(doc_ids, "seq", axis=0, tiled=True)
     key_pos = jnp.arange(keys.shape[0], dtype=jnp.int32)
     key_heads = to_heads(keys)

time: 137 us -> 146 us (1.066)
  waiting for transfers between devices: 30.7 us -> 68.3 us
  blocking collectives: 80.5 us -> 47.3 us
  starting transfers between devices: 0.04 us -> 3.16 us
  local copies, waits for them, and re-layouts: 2.12 us -> 3.69 us
    ppermute x0 -> x7, waiting for transfers between devices: none -> 45.4 us  [ring_gather(): blocks.append(lax.ppermute(blocks[-1], axis, ahead))]
    all_gather x1 -> x0, blocking collectives: 33.8 us -> none  [shards(): values = lax.all_gather(value_states, 'seq', axis=0, tiled=True)]
    all_gather x1, waiting for transfers between devices: 5.75 us -> 0.02 us  [shards(): lax.all_gather(out_weight, 'seq', axis=1, tiled=True)]
    ppermute x0 -> x7, starting transfers between devices: none -> 3.12 us  [ring_gather(): blocks.append(lax.ppermute(blocks[-1], axis, ahead))]
    reduce_scatter x1, waiting for transfers between devices: 24.2 us -> 22.2 us  [shards(): summed = lax.psum_scatter(mapped, 'head', scatter_dimension=1, tiled=True)]
    unnamed x5 -> x12, local copies, waits for them, and re-layouts: 2.11 us -> 2.98 us
  transfers between devices with their start and end apart: 2 -> 9, of which waited for: 2 -> 7; matrix products, arithmetic and copies ran while one was open for 4% -> 5% of each run, Pallas kernels for 0% -> 0%
where the time goes in v1:
time: 146 us
  waiting for transfers between devices  68.3 us (47%)
  blocking collectives  47.3 us (32%)
  between operations  14.7 us (10%)
  matrix products  5.61 us (4%)
  local copies, waits for them, and re-layouts  3.69 us (3%)
  other arithmetic  3.29 us (2%)
  starting transfers between devices  3.16 us (2%)
    ppermute x7, waiting for transfers between devices, ring_gather(): blocks.append(lax.ppermute(blocks[-1], axis, ahead))  45.4 us
    all_gather x1, blocking collectives, shards(): keys = lax.all_gather(key_states, 'seq', axis=0, tiled=True)  33.6 us
    reduce_scatter x1, waiting for transfers between devices, shards(): summed = lax.psum_scatter(mapped, 'head', scatter_dimension=1, tiled=True)  22.2 us
    unnamed x1, blocking collectives  13.7 us
    dot_general x1, matrix products, shards(): jnp.dot(attended, lax.all_gather(out_weight, 'seq', axis=1, tiled=True),...  4.09 us
    ppermute x7, starting transfers between devices, ring_gather(): blocks.append(lax.ppermute(blocks[-1], axis, ahead))  3.12 us
    unnamed x12, local copies, waits for them, and re-layouts  2.98 us
  transfers between devices with their start and end apart: 9, of which 7 were waited for; matrix products, arithmetic and copies ran while one was open for 5% of the time, Pallas kernels for 0%

profile of v1, /device:TPU:0, one launch (start us, length us, event | category | flops | bytes accessed | tf_op | source)
XLA Modules:
  0.0 146.2 jit_solution(6923606614684664150)
XLA Ops:
  6.5 0.0 all-gather.2.cloned.1.call-start
  6.5 0.7 all-gather.2.cloned.1.call-update
  7.3 0.0 reduce-scatter.2.cloned.1.call-start
  7.3 3.0 %collective-permute-start = (bf16[64,512]{1,0:T(8,128)(2,1)}, bf16[64,512]{1,0:T(8,128)(2,1)S(1)}, u32[]{:S(2)}, u32[]{:S(2)}) collective-permute-start(bf16[64,512]{1,0:T(8,128)(2,1)} %param.10), channel_id=1, source_target_pairs={{0,4},{4,8},{8,12},{12,16},{16,20},{20,24},{24,28},{28,0},{1,5},{5... | collective-permute-start | bytes 196616 | tf_op jit(solution)/shard_map/ppermute | solution.py:21
  10.3 0.6 fusion.22
  11.6 1.2 dynamic-slice
  13.5 0.9 dynamic-update-slice
  14.3 13.7 %all-reduce = s32[512]{0:T(512)S(1)} all-reduce(s32[512]{0:T(512)S(1)} %dynamic-update-slice), channel_id=1, replica_groups=mesh['seq'=8,'head'=4] {'seq'}, use_global_device_ids=true, to_apply=%add | all-reduce | flops 512 | bytes 4096
  28.0 0.8 bitcast_dynamic-update-slice_fusion.7
  28.9 33.6 %all_gather.10 = bf16[512,512]{1,0:T(8,128)(2,1)S(1)} all-gather(bf16[64,512]{1,0:T(8,128)(2,1)} %param.9), channel_id=1, replica_groups=mesh['seq'=8,'head'=4] {'seq'}, dimensions={0}, use_global_device_ids=true | all-gather | bytes 589824 | tf_op jit(solution)/shard_map/all_gather | solution.py:65
  62.5 0.0 collective-permute-done
  62.5 0.1 collective-permute-start.1
  62.6 7.0 %collective-permute-done.1 = bf16[64,512]{1,0:T(8,128)(2,1)S(1)} collective-permute-done((bf16[64,512]{1,0:T(8,128)(2,1)S(1)}, bf16[64,512]{1,0:T(8,128)(2,1)S(1)}, u32[]{:S(2)}, u32[]{:S(2)}) %collective-permute-start.1) | collective-permute-done | bytes 65568 | tf_op jit(solution)/shard_map/ppermute | solution.py:21
  69.6 0.0 collective-permute-start.2
  69.7 8.5 %collective-permute-done.2 = bf16[64,512]{1,0:T(8,128)(2,1)S(1)} collective-permute-done((bf16[64,512]{1,0:T(8,128)(2,1)S(1)}, bf16[64,512]{1,0:T(8,128)(2,1)S(1)}, u32[]{:S(2)}, u32[]{:S(2)}) %collective-permute-start.2) | collective-permute-done | bytes 65568 | tf_op jit(solution)/shard_map/ppermute | solution.py:21
  78.1 0.0 collective-permute-start.3
  78.1 7.1 %collective-permute-done.3 = bf16[64,512]{1,0:T(8,128)(2,1)S(1)} collective-permute-done((bf16[64,512]{1,0:T(8,128)(2,1)S(1)}, bf16[64,512]{1,0:T(8,128)(2,1)S(1)}, u32[]{:S(2)}, u32[]{:S(2)}) %collective-permute-start.3) | collective-permute-done | bytes 65568 | tf_op jit(solution)/shard_map/ppermute | solution.py:21
  85.3 0.0 collective-permute-start.4
  85.3 8.8 %collective-permute-done.4 = bf16[64,512]{1,0:T(8,128)(2,1)S(1)} collective-permute-done((bf16[64,512]{1,0:T(8,128)(2,1)S(1)}, bf16[64,512]{1,0:T(8,128)(2,1)S(1)}, u32[]{:S(2)}, u32[]{:S(2)}) %collective-permute-start.4) | collective-permute-done | bytes 65568 | tf_op jit(solution)/shard_map/ppermute | solution.py:21
  94.1 0.0 collective-permute-start.5
  94.1 7.0 %collective-permute-done.5 = bf16[64,512]{1,0:T(8,128)(2,1)S(1)} collective-permute-done((bf16[64,512]{1,0:T(8,128)(2,1)S(1)}, bf16[64,512]{1,0:T(8,128)(2,1)S(1)}, u32[]{:S(2)}, u32[]{:S(2)}) %collective-permute-start.5) | collective-permute-done | bytes 65568 | tf_op jit(solution)/shard_map/ppermute | solution.py:21
  101.1 0.0 collective-permute-start.6
  101.1 7.0 %collective-permute-done.6 = bf16[64,512]{1,0:T(8,128)(2,1)S(1)} collective-permute-done((bf16[64,512]{1,0:T(8,128)(2,1)S(1)}, bf16[64,512]{1,0:T(8,128)(2,1)S(1)}, u32[]{:S(2)}, u32[]{:S(2)}) %collective-permute-start.6) | collective-permute-done | bytes 65568 | tf_op jit(solution)/shard_map/ppermute | solution.py:21
  108.0 3.3 %conditional.1 = (f32[4,64]{1,0:T(4,128)S(1)}, f32[4,64,128]{2,1,0:T(8,128)S(1)}) conditional(s32[]{:T(128)} %convert_element_type.22, () %tuple.13, (s32[512]{0:T(512)S(1)}, s32[64]{0:T(128)S(1)}, s32[512]{0:T(512)S(1)}, s32[64]{0:T(128)}, bf16[64,512]{1,0:T(8,128)(2,1)}, /*index=5*/bf16[512,512]{1,0:T(8,128)(2,1)S(1)}, ...), branch_computations={%region_1.2_spmd, %region_2.5_spmd.clone.clone} | conditional | flops 68387664 | bytes 5061336 | solution.py:83
  108.1 0.8 compare_and_fusion
  108.8 1.2 fusion.23
  110.1 0.6 gather_fusion
  110.7 0.1 reshape_reshape.5
  110.8 0.3 fusion.3
  111.1 0.2 fusion.6
  111.3 0.0 copy-start
  111.4 0.0 all-gather.2.cloned.1.call-done
  111.4 4.1 %fusion.16 = f32[64,4096]{1,0:T(8,128)} fusion(bf16[512,4096]{1,0:T(8,128)(2,1)} %all-gather.2.cloned.1.call-done, f32[4,64,128]{2,1,0:T(8,128)S(1)} %get-tuple-element.45, f32[4,64]{1,0:T(4,128)S(1)} %get-tuple-element.46), kind=kOutput, calls=%fused_computation.26 | convolution fusion | flops 268500992 | bytes 5374976 | tf_op jit(solution)/shard_map/dot_general | solution.py:94
  115.5 0.0 reduce-scatter.2.cloned.1.call-update
  115.5 22.2 %reduce-scatter.2.cloned.1.call-done = f32[64,1024]{1,0:T(8,128)} async-done(((f32[64,4096]{1,0:T(8,128)}), f32[64,1024]{1,0:T(8,128)}) %reduce-scatter.2.cloned.1.call-update) | async-done | bytes 262160 | tf_op jit(solution)/shard_map/reduce_scatter | solution.py:99
  137.7 0.0 copy-done
  137.7 1.6 %add_convert_fusion = bf16[64,1024]{1,0:T(8,128)(2,1)} fusion(f32[64,1024]{1,0:T(8,128)} %reduce-scatter.2.cloned.1.call-done, bf16[64,1024]{1,0:T(8,128)(2,1)S(1)} %copy-done), kind=kLoop, calls=%fused_computation.24 | loop fusion | flops 196608 | bytes 524288 | tf_op jit(solution)/shard_map/convert_element_type | solution.py:100
  (16 shorter events, 0.1 us)
Async XLA Ops:
  6.5 104.8 %all-gather.2.cloned.1.call-start = ((), (), s32[]{:S(2)}) async-start(), calls=%async_computation.1 | async-start | bytes 4718592 | tf_op jit(solution)/shard_map/all_gather | solution.py:96
  7.3 130.5 %reduce-scatter.2.cloned.1.call-start = ((), (), s32[]{:S(2)}) async-start(), calls=%async_computation.2 | async-start | bytes 1310720 | tf_op jit(solution)/shard_map/reduce_scatter | solution.py:99
  7.3 55.2 %collective-permute-start = (bf16[64,512]{1,0:T(8,128)(2,1)}, bf16[64,512]{1,0:T(8,128)(2,1)S(1)}, u32[]{:S(2)}, u32[]{:S(2)}) collective-permute-start(bf16[64,512]{1,0:T(8,128)(2,1)} %param.10), channel_id=1, source_target_pairs={{0,4},{4,8},{8,12},{12,16},{16,20},{20,24},{24,28},{28,0},{1,5},{5... | collective-permute-start | bytes 196616 | tf_op jit(solution)/shard_map/ppermute | solution.py:21
  62.5 7.1 %collective-permute-start.1 = (bf16[64,512]{1,0:T(8,128)(2,1)S(1)}, bf16[64,512]{1,0:T(8,128)(2,1)S(1)}, u32[]{:S(2)}, u32[]{:S(2)}) collective-permute-start(bf16[64,512]{1,0:T(8,128)(2,1)S(1)} %collective-permute-done), channel_id=1, source_target_pairs={{0,4},{4,8},{8,12},{12,16},{16,20},{20,24},{24,28},{28,0},{1,5},{5... | collective-permute-start | bytes 196616 | tf_op jit(solution)/shard_map/ppermute | solution.py:21
  69.6 8.5 %collective-permute-start.2 = (bf16[64,512]{1,0:T(8,128)(2,1)S(1)}, bf16[64,512]{1,0:T(8,128)(2,1)S(1)}, u32[]{:S(2)}, u32[]{:S(2)}) collective-permute-start(bf16[64,512]{1,0:T(8,128)(2,1)S(1)} %collective-permute-done.1), channel_id=1, source_target_pairs={{0,4},{4,8},{8,12},{12,16},{16,20},{20,24},{24,28},{28,0},{1,5},{5... | collective-permute-start | bytes 196616 | tf_op jit(solution)/shard_map/ppermute | solution.py:21
  78.1 7.1 %collective-permute-start.3 = (bf16[64,512]{1,0:T(8,128)(2,1)S(1)}, bf16[64,512]{1,0:T(8,128)(2,1)S(1)}, u32[]{:S(2)}, u32[]{:S(2)}) collective-permute-start(bf16[64,512]{1,0:T(8,128)(2,1)S(1)} %collective-permute-done.2), channel_id=1, source_target_pairs={{0,4},{4,8},{8,12},{12,16},{16,20},{20,24},{24,28},{28,0},{1,5},{5... | collective-permute-start | bytes 196616 | tf_op jit(solution)/shard_map/ppermute | solution.py:21
  85.3 8.8 %collective-permute-start.4 = (bf16[64,512]{1,0:T(8,128)(2,1)S(1)}, bf16[64,512]{1,0:T(8,128)(2,1)S(1)}, u32[]{:S(2)}, u32[]{:S(2)}) collective-permute-start(bf16[64,512]{1,0:T(8,128)(2,1)S(1)} %collective-permute-done.3), channel_id=1, source_target_pairs={{0,4},{4,8},{8,12},{12,16},{16,20},{20,24},{24,28},{28,0},{1,5},{5... | collective-permute-start | bytes 196616 | tf_op jit(solution)/shard_map/ppermute | solution.py:21
  94.1 7.0 %collective-permute-start.5 = (bf16[64,512]{1,0:T(8,128)(2,1)S(1)}, bf16[64,512]{1,0:T(8,128)(2,1)S(1)}, u32[]{:S(2)}, u32[]{:S(2)}) collective-permute-start(bf16[64,512]{1,0:T(8,128)(2,1)S(1)} %collective-permute-done.4), channel_id=1, source_target_pairs={{0,4},{4,8},{8,12},{12,16},{16,20},{20,24},{24,28},{28,0},{1,5},{5... | collective-permute-start | bytes 196616 | tf_op jit(solution)/shard_map/ppermute | solution.py:21
  101.1 7.0 %collective-permute-start.6 = (bf16[64,512]{1,0:T(8,128)(2,1)S(1)}, bf16[64,512]{1,0:T(8,128)(2,1)S(1)}, u32[]{:S(2)}, u32[]{:S(2)}) collective-permute-start(bf16[64,512]{1,0:T(8,128)(2,1)S(1)} %collective-permute-done.5), channel_id=1, source_target_pairs={{0,4},{4,8},{8,12},{12,16},{16,20},{20,24},{24,28},{28,0},{1,5},{5... | collective-permute-start | bytes 196616 | tf_op jit(solution)/shard_map/ppermute | solution.py:21
  111.3 26.4 %copy-start = (bf16[64,1024]{1,0:T(8,128)(2,1)S(1)}, bf16[64,1024]{1,0:T(8,128)(2,1)}, u32[]{:S(2)}) copy-start(bf16[64,1024]{1,0:T(8,128)(2,1)} %param.13) | copy-start | bytes 393220
Sparse Core Ops, SparseCore 0:
  9.4 84.8 all-gather.1
  115.6 22.0 reduce-scatter.1
